TPU v7x, 256 devices: a whole 4x4x8 slice. The times are simulated.
256 devices in a mesh: role: 2 (over z_hi), dp: 16 (over y, z_lo), mp: 8 (over x, core).
Axes of the slice: x: 4, y: 4, z: 8 (z_hi: 2, z_lo: 4; z = z_hi * 4 + z_lo), core: 2. Of those that a mesh axis runs over, the one named last changes fastest.
Arguments:
- patches: bfloat16 [25088, 1280], P('dp', 'mp'), may hold values from -6 to 6
- pred_states: bfloat16 [16384, 384], P('dp'), may hold values from -6 to 6
- ema_up: bfloat16 [1280, 5120], P(('role', 'dp'), 'mp'), may hold values from -0.15625 to 0.15625
- ema_down: bfloat16 [5120, 1280], P('mp', ('role', 'dp')), may hold values from -0.078125 to 0.078125
- pred_up: bfloat16 [384, 1536], P(('role', 'dp'), 'mp'), may hold values from -0.3125 to 0.3125
- pred_down: bfloat16 [1536, 384], P('mp', ('role', 'dp')), may hold values from -0.15625 to 0.15625
- pred_out: bfloat16 [384, 1280], P(('role', 'dp'), 'mp'), may hold values from -0.3125 to 0.3125
- masked_index: int32 [16, 1024], P('dp'), may hold values from 0 to 1567, as said below
- masked_count: int32 [16], P('dp'), may hold values from 512 to 1024, as said below
- loss_scale: float32 [], replicated, may hold values from 81920 to 327680
Outputs:
- loss: float32 [], replicated
- grad_up: float32 [384, 1536], P(('role', 'dp'), 'mp')
- grad_down: float32 [1536, 384], P('mp', ('role', 'dp'))
- grad_out: float32 [384, 1280], P(('role', 'dp'), 'mp')
Inputs may be any that keep to these rules, and one draw needn't show every extreme that they name: `masked_index`: within a clip the slots name distinct tokens; the slots below masked_count name the masked tokens, which are whole tubes: all 8 frames (token f * 196 + s for frame f) of some spatial positions s. Slots from masked_count on name other tokens and are ignored. `masked_count`: each count is 8 times a whole number; some clip has exactly 1024.
All inputs are finite; a program needn't handle non-finite values.
Results may differ from a plain program's by a relative error of at most 0.012.
Values may be sent and summed in bfloat16 or wider, within the bound.
No kernel may reach another device: no remote copies, remote signals or barrier semaphores. Data moves between devices by JAX's collectives and lax.ppermute only.
A program may use at most 128 MiB of HBM per device.

v0:
```python
import functools
import jax
import jax.numpy as jnp
from jax import lax
from jax.sharding import Mesh
from jax.sharding import PartitionSpec as P

D = 1280
TOK = 1568
MMAX = 1024
MP = ("mp_0", "mp_1")
ROLE_DP = ("role", "dp_0", "dp_1")
DP = ("dp_0", "dp_1")
ROLE_DP_MP = ("role", "dp_0", "dp_1", "mp_0", "mp_1")
EPS = 1e-06
COEF = 0.7978845608028654


def joined_along(pieces, dim):
    pieces = jnp.moveaxis(pieces, 0, dim)
    lengths = pieces.shape
    return pieces.reshape(*lengths[:dim], lengths[dim] * lengths[dim + 1], *lengths[dim + 2 :])


def from_everyone(shard, axis):
    copies = jnp.broadcast_to(shard, (lax.axis_size(axis), *shard.shape))
    return lax.all_to_all(copies, axis, split_axis=0, concat_axis=0, tiled=True)


def gather_directly(shard, axis, dim):
    return joined_along(from_everyone(shard, axis), dim)


def of_everyone(shard, axis):
    return from_everyone(shard, axis).sum(axis=0)


def in_one(arrays, axis):
    vector, at, outs = (jnp.concatenate([a.reshape(-1) for a in arrays]), 0, [])
    total = of_everyone(vector, axis)
    for a in arrays:
        outs.append(total[at : at + a.size].reshape(a.shape))
        at += a.size
    return tuple(outs)


def passed_along(block, axis, distance):
    devices = range(lax.axis_size(axis))
    route = [(i - distance, i) for i in devices if i - distance in devices]
    return lax.ppermute(block, axis, route)


def sent_together(arrays, axis, dim, along):
    widths = [a.shape[along] for a in arrays]
    both = jnp.concatenate(arrays, axis=along)
    filled = lax.all_gather(both, axis, axis=dim, tiled=True)
    return tuple(jnp.split(filled, [sum(widths[:k]) for k in range(1, len(widths))], axis=along))


def by_axis(shard, axes):
    return functools.reduce(lax.psum, axes, shard)


def filled_up(lines, devices):
    spare = -len(lines) % devices
    return jnp.pad(lines, [(0, spare)] + [(0, 0)] * (lines.ndim - 1))


def sum_by_parts(shard, axis):
    lines = shard.reshape(-1, *shard.shape[1:][-1:])
    own = lax.psum_scatter(
        filled_up(lines, lax.axis_size(axis)), axis, scatter_dimension=0, tiled=True
    )
    whole = lax.all_gather(own, axis).reshape(-1, *lines.shape[1:])
    return lax.slice_in_dim(whole, 0, len(lines)).reshape(shard.shape)


def cut_along(shard, dim, devices):
    before, after = (shard.shape[:dim], shard.shape[dim + 1 :])
    return jnp.moveaxis(shard.reshape(*before, devices, -1, *after), dim, 0)


def sum_together(arrays, axis, dims):
    devices = lax.axis_size(axis)
    pieces = [cut_along(a, dim, devices) for a, dim in zip(arrays, dims)]
    lines = jnp.concatenate([b.reshape(devices, -1) for b in pieces], axis=1)
    width = max(16, -(-lines.shape[1] // 1024) * 8)
    lines = jnp.pad(lines, ((0, 0), (0, width * 128 - lines.shape[1]))).reshape(-1, 128)
    vector, at, outs = (lax.psum_scatter(lines, axis, tiled=True).reshape(-1), 0, [])
    for b in pieces:
        part = b[0]
        outs.append(vector[at : at + part.size].reshape(part.shape))
        at += part.size
    return tuple(outs)


def summed_on_arrival(shard, axis, dim):
    pieces = cut_along(shard, dim, lax.axis_size(axis))
    arrived = lax.all_to_all(pieces, axis, split_axis=0, concat_axis=0, tiled=True)
    return arrived.sum(axis=0)


def normalize(values):
    row_mean = jnp.mean(values, axis=-1, keepdims=True)
    row_deviations = values - row_mean
    variance = jnp.mean(row_deviations * row_deviations, axis=-1, keepdims=True)
    return row_deviations * lax.rsqrt(variance + EPS)


def gelu_slope(values):
    inner = COEF * (values + 0.044715 * values * values * values)
    tangent = jnp.tanh(inner)
    return 0.5 * (1.0 + tangent) + 0.5 * values * (1.0 - tangent * tangent) * COEF * (
        1.0 + 3.0 * 0.044715 * values * values
    )


def pick_rows(source_table, token_index):
    clip_count = token_index.shape[0]
    slot_total = token_index.shape[1]
    clip_grid = source_table.reshape(clip_count, TOK, source_table.shape[1])
    onehot = (token_index[:, :, None] == jnp.arange(TOK, dtype=jnp.int32)[None, None, :]).astype(
        jnp.bfloat16
    )
    picked = jnp.einsum("ckt,ctw->ckw", onehot, clip_grid, preferred_element_type=jnp.float32)
    return picked.astype(jnp.bfloat16).reshape(clip_count * slot_total, source_table.shape[1])


def body(
    patches,
    pred_states,
    ema_up,
    ema_down,
    pred_up,
    pred_down,
    pred_out,
    masked_index,
    masked_count,
    loss_scale,
):
    role_index = lax.axis_index("role")
    clip_count = masked_index.shape[0]
    feat_width = float(D)
    half_slots = MMAX // 2
    half_index = lax.dynamic_slice_in_dim(masked_index, role_index * half_slots, half_slots, 1)
    own_rows = pick_rows(patches, half_index)
    whole_rows = gather_directly(own_rows, MP, 1)
    working = role_index >= 0
    block_rows = own_rows.shape[0]
    up_cols = lax.all_gather(ema_up, ROLE_DP, axis=0, tiled=True)
    down_rows = lax.all_gather(ema_down, ROLE_DP, axis=1, tiled=True)

    def encode_block():
        normed = normalize(whole_rows.astype(jnp.float32)).astype(jnp.bfloat16)
        hidden = jax.nn.gelu(
            jnp.dot(normed, up_cols, preferred_element_type=jnp.float32), approximate=True
        ).astype(jnp.bfloat16)
        return jnp.dot(hidden, down_rows, preferred_element_type=jnp.float32)

    def skip_block():
        return jnp.zeros((block_rows, whole_rows.shape[1]), jnp.float32)

    partial_sum = lax.cond(working, encode_block, skip_block)
    branch = lax.psum_scatter(partial_sum, MP, scatter_dimension=1, tiled=True)
    block_out = own_rows.astype(jnp.float32) + branch
    first_sum, second_sum = in_one(
        (
            jnp.sum(block_out, axis=-1, keepdims=True),
            jnp.sum(block_out * block_out, axis=-1, keepdims=True),
        ),
        MP,
    )
    row_mean = first_sum / feat_width
    row_deviations = block_out - row_mean
    variance = second_sum / feat_width - row_mean * row_mean
    target_all = (row_deviations * lax.rsqrt(variance + EPS)).astype(jnp.bfloat16)
    local_width = target_all.shape[1]
    earlier = passed_along(target_all, "role", 1)
    joined = jnp.concatenate(
        (
            earlier.reshape(clip_count, half_slots, local_width),
            target_all.reshape(clip_count, half_slots, local_width),
        ),
        axis=1,
    )
    targets = joined.reshape(clip_count * MMAX, local_width)
    up_rows, out_rows = sent_together((pred_up, pred_out), ROLE_DP, 0, 1)
    down_cols = gather_directly(pred_down, ROLE_DP, 1)
    total = of_everyone(jnp.sum(masked_count).astype(jnp.float32), DP)
    states = pred_states.astype(jnp.float32)
    pnormed = normalize(states).astype(jnp.bfloat16)
    preact = jnp.dot(pnormed, up_rows, preferred_element_type=jnp.float32)
    hid_act = jax.nn.gelu(preact, approximate=True).astype(jnp.bfloat16)
    mixer_out = lax.psum(jnp.dot(hid_act, down_cols, preferred_element_type=jnp.float32), MP)
    updated = states + mixer_out
    row_mean_p = jnp.mean(updated, axis=-1, keepdims=True)
    predictor_deviations = updated - row_mean_p
    reciprocal_spread = lax.rsqrt(
        jnp.mean(predictor_deviations * predictor_deviations, axis=-1, keepdims=True) + EPS
    )
    standardized_input = predictor_deviations * reciprocal_spread
    output_normalized = standardized_input.astype(jnp.bfloat16)
    predicted = jnp.dot(output_normalized, out_rows, preferred_element_type=jnp.float32)
    live_mask = (
        (jnp.arange(MMAX, dtype=jnp.int32)[None, :] < masked_count[:, None])
        .astype(jnp.float32)
        .reshape(clip_count * MMAX, 1)
    )
    predictor_side = (role_index == 1).astype(jnp.float32)
    norm_scale = total * feat_width
    residue = predicted - targets.astype(jnp.float32)
    smooth = jnp.sqrt(residue * residue + 1.0)
    local_loss = jnp.sum(live_mask * (smooth - 1.0)) * predictor_side
    loss = by_axis(local_loss, ROLE_DP_MP) / norm_scale
    grad_pred = (loss_scale * live_mask * residue / smooth / norm_scale * predictor_side).astype(
        jnp.bfloat16
    )
    normalized_gradient = sum_by_parts(
        jnp.einsum("rd,kd->rk", grad_pred, out_rows, preferred_element_type=jnp.float32), MP
    )
    gradient_update = reciprocal_spread * (
        normalized_gradient
        - jnp.mean(normalized_gradient, axis=-1, keepdims=True)
        - standardized_input
        * jnp.mean(normalized_gradient * standardized_input, axis=-1, keepdims=True)
    )
    gradient_update = gradient_update.astype(jnp.bfloat16)
    down_local = jnp.einsum(
        "rf,rk->fk", hid_act, gradient_update, preferred_element_type=jnp.float32
    )
    grad_act = jnp.einsum(
        "rk,fk->rf", gradient_update, down_cols, preferred_element_type=jnp.float32
    )
    grad_pre = (grad_act * gelu_slope(preact)).astype(jnp.bfloat16)
    up_local = jnp.einsum("rk,rf->kf", pnormed, grad_pre, preferred_element_type=jnp.float32)
    out_local = jnp.einsum(
        "rk,rd->kd", output_normalized, grad_pred, preferred_element_type=jnp.float32
    )
    grad_up, grad_out = tuple(
        (
            part.astype(jnp.float32)
            for part in sum_together(
                (up_local.astype(jnp.bfloat16), out_local.astype(jnp.bfloat16)), ROLE_DP, (0, 0)
            )
        )
    )
    grad_down = summed_on_arrival(down_local, ROLE_DP, 1)
    return (loss, grad_up, grad_down, grad_out)


def solution(mesh):
    finer = Mesh(
        mesh.devices.reshape(mesh.shape["role"], 4, 4, 4, 2),
        ("role", "dp_0", "dp_1", "mp_0", "mp_1"),
    )
    return jax.shard_map(
        body,
        mesh=finer,
        in_specs=(
            P(DP, MP),
            P(DP, None),
            P(ROLE_DP, MP),
            P(MP, ROLE_DP),
            P(ROLE_DP, MP),
            P(MP, ROLE_DP),
            P(ROLE_DP, MP),
            P(DP, None),
            P(DP),
            P(),
        ),
        out_specs=(P(), P(ROLE_DP, MP), P(MP, ROLE_DP), P(ROLE_DP, MP)),
        check_vma=False,
    )
```

profile of v0, /device:TPU:2, one launch (start us, length us, event | category | flops | bytes accessed | tf_op | source)
XLA Modules:
  0.0 619.0 jit_solution(12182839815354292576)
XLA Ops:
  10.9 11.5 %all-to-all-start = ((bf16[32,192,12]{1,2,0:T(8,128)(2,1)}), bf16[32,192,12]{1,2,0:T(8,128)(2,1)S(1)}, u32[]{:S(2)}, u32[]{:S(2)}) async-start(bf16[32,192,12]{1,2,0:T(8,128)(2,1)} %broadcast_in_dim.10), calls=%async_computation | async-start | bytes 524288 | tf_op jit(solution)/shard_map/all_to_all | solution.py:27
  23.2 75.8 %all-gather.1 = bf16[32,12,352]{2,1,0:T(8,128)(2,1)S(1)} all-gather(bf16[1,12,352]{2,1,0:T(8,128)(2,1)S(1)} %maximum_bitcast_fusion.1), channel_id=1, replica_groups=mesh['role'=2,'dp_0'=4,'dp_1'=4,'mp_0'=4,'mp_1'=2] {'role','dp_0','dp_1'}, dimensions={0}, use_global_device_ids=true | all-gather | bytes 278784 | tf_op jit(solution)/shard_map/all_gather | solution.py:56
  102.9 4.8 all-to-all-start.1
  113.9 11.1 %all-to-all-done.1 = bf16[8,512,160]{1,2,0:T(8,128)(2,1)S(1)} async-done(((bf16[8,512,160]{1,2,0:T(8,128)(2,1)}), bf16[8,512,160]{1,2,0:T(8,128)(2,1)S(1)}, u32[]{:S(2)}, u32[]{:S(2)}) %all-to-all-start.1) | async-done | bytes 1310752 | tf_op jit(solution)/shard_map/all_to_all | solution.py:27
  124.9 32.0 %all-gather.6.cloned.1.call-done = bf16[1280,640]{1,0:T(8,128)(2,1)} async-done(((bf16[40,640]{1,0:T(8,128)(2,1)}), bf16[1280,640]{1,0:T(8,128)(2,1)}) %all-gather.6.cloned.1.call-update) | async-done | bytes 1638416 | tf_op jit(solution)/shard_map/all_gather | solution.py:150
  156.9 142.1 %all-gather.8.cloned.1.call-done = bf16[640,1280]{0,1:T(8,128)(2,1)} async-done(((bf16[640,40]{0,1:T(8,128)(2,1)}), bf16[640,1280]{0,1:T(8,128)(2,1)}) %all-gather.8.cloned.1.call-update) | async-done | bytes 1638416 | tf_op jit(solution)/shard_map/all_gather | solution.py:151
  299.0 8.5 %conditional.1 = (f32[512,1280]{1,0:T(8,128)}) conditional(s32[]{:T(128)} %convert_element_type.101, () %tuple.14, (bf16[512,8,160]{0,2,1:T(8,128)(2,1)S(1)}, bf16[1280,640]{1,0:T(8,128)(2,1)}, bf16[640,1280]{0,1:T(8,128)(2,1)}) %tuple.41), branch_computations={%region_5.0_spmd, %region_6.9_spmd} | conditional | flops 1687224832 | bytes 12470280 | solution.py:163
  301.1 6.4 %fusion.10 = f32[512,1280]{1,0:T(8,128)} fusion(bf16[640,1280]{0,1:T(8,128)(2,1)} %get-tuple-element.25, bf16[512,1280]{0,1:T(8,128)(2,1)} %fusion.1, bf16[1280,640]{1,0:T(8,128)(2,1)} %get-tuple-element.11), kind=kOutput, calls=%fused_computation.14 | convolution fusion | flops 1680670720 | bytes 7208960 | tf_op jit(solution)/shard_map/cond/branch_1_fun/dot_general | solution.py:158
  307.5 3.2 copy.34
  312.0 5.7 all-to-all-start.3
  318.4 7.2 %all-to-all-done.3 = f32[16,1,1]{2,1,0:T(1,128)S(1)} async-done(((f32[16,1,1]{2,1,0:T(1,128)}), f32[16,1,1]{2,1,0:T(1,128)S(1)}, u32[]{:S(2)}, u32[]{:S(2)}) %all-to-all-start.3) | async-done | bytes 96 | tf_op jit(solution)/shard_map/all_to_all | solution.py:27
  329.3 13.2 %reduce-scatter.3.cloned.1.call-done = f32[512,160]{0,1:T(8,128)} async-done(((f32[512,1280]{0,1:T(8,128)}), f32[512,160]{0,1:T(8,128)}) %reduce-scatter.3.cloned.1.call-update) | async-done | bytes 327696 | tf_op jit(solution)/shard_map/reduce_scatter | solution.py:164
  344.2 7.0 %all-to-all-start.2 = ((f32[8,1,1024]{2,1,0:T(1,128)}), f32[8,1,1024]{2,1,0:T(1,128)S(1)}, u32[]{:S(2)}, u32[]{:S(2)}) async-start(f32[8,1,1024]{2,1,0:T(1,128)} %broadcast_in_dim.12), calls=%async_computation.3 | async-start | bytes 65536 | tf_op jit(solution)/shard_map/all_to_all | solution.py:27
  351.2 4.0 all-to-all-done.2
  356.3 7.8 %collective-permute-start = (bf16[512,160]{0,1:T(8,128)(2,1)S(1)}, bf16[512,160]{0,1:T(8,128)(2,1)S(1)}, u32[]{:S(2)}, u32[]{:S(2)}) collective-permute-start(bf16[512,160]{0,1:T(8,128)(2,1)S(1)} %multiply_convert_fusion.2), channel_id=1, source_target_pairs={{0,128},{1,129},{2,130},{3,131},{4,132},{5,133},{6,134},{7,135},{8... | collective-permute-start | bytes 491528 | tf_op jit(solution)/shard_map/ppermute | solution.py:50
  371.0 36.0 %reduce-scatter.5.cloned.1.call-done = f32[128,384]{1,0:T(8,128)} async-done(((f32[1024,384]{1,0:T(8,128)}), f32[128,384]{1,0:T(8,128)}) %reduce-scatter.5.cloned.1.call-update) | async-done | bytes 196624 | tf_op jit(solution)/shard_map/reduce_scatter | solution.py:71
  408.8 27.1 %all-gather.10.cloned.1.call-done = f32[1024,384]{1,0:T(8,128)} async-done(((f32[128,384]{1,0:T(8,128)}), f32[1024,384]{1,0:T(8,128)}) %all-gather.10.cloned.1.call-update) | async-done | bytes 1572880 | tf_op jit(solution)/shard_map/all_gather | solution.py:74
  444.4 10.0 %all-to-all-start.4 = ((f32[32,192,12]{1,2,0:T(8,128)}), f32[32,192,12]{1,2,0:T(8,128)S(1)}, u32[]{:S(2)}, u32[]{:S(2)}) async-start(f32[32,192,12]{1,2,0:T(8,128)} %bitcast.9), calls=%async_computation.6 | async-start | bytes 1048576 | tf_op jit(solution)/shard_map/all_to_all | solution.py:99
  456.4 16.2 %psum.43 = f32[]{:T(128)} all-reduce(f32[]{:T(128)S(6)} %mul.192), channel_id=1, replica_groups=mesh['role'=2,'dp_0'=4,'dp_1'=4,'mp_0'=4,'mp_1'=2] {'role'}, use_global_device_ids=true, to_apply=%region_14.0 | all-reduce | flops 1 | bytes 8 | tf_op jit(solution)/shard_map/psum | solution.py:61
  472.6 10.4 %psum.44 = f32[]{:T(128)} all-reduce(f32[]{:T(128)} %psum.43), channel_id=1, replica_groups=mesh['role'=2,'dp_0'=4,'dp_1'=4,'mp_0'=4,'mp_1'=2] {'dp_0'}, use_global_device_ids=true, to_apply=%region_15.0 | all-reduce | flops 1 | bytes 8 | tf_op jit(solution)/shard_map/psum | solution.py:61
  483.6 10.3 %psum.45 = f32[]{:T(128)} all-reduce(f32[]{:T(128)} %psum.44), channel_id=1, replica_groups=mesh['role'=2,'dp_0'=4,'dp_1'=4,'mp_0'=4,'mp_1'=2] {'dp_1'}, use_global_device_ids=true, to_apply=%region_16.0 | all-reduce | flops 1 | bytes 8 | tf_op jit(solution)/shard_map/psum | solution.py:61
  494.5 10.4 %psum.46 = f32[]{:T(128)} all-reduce(f32[]{:T(128)} %psum.45), channel_id=1, replica_groups=mesh['role'=2,'dp_0'=4,'dp_1'=4,'mp_0'=4,'mp_1'=2] {'mp_0'}, use_global_device_ids=true, to_apply=%region_17.0 | all-reduce | flops 1 | bytes 8 | tf_op jit(solution)/shard_map/psum | solution.py:61
  504.9 3.1 psum.47
  508.6 98.4 %all-reduce.7.cloned.1.call-done = bf16[1280,128]{1,0:T(8,128)(2,1)} async-done(((bf16[1280,128]{1,0:T(8,128)(2,1)}), bf16[1280,128]{1,0:T(8,128)(2,1)}) %all-reduce.7.cloned.1.call-update) | async-done | bytes 327696
  (104 shorter events, 44.5 us)
Async XLA Ops:
  8.0 92.6 %copy-start = (bf16[1568,160]{0,1:T(8,128)(2,1)S(1)}, bf16[1568,160]{0,1:T(8,128)(2,1)}, u32[]{:S(2)}) copy-start(bf16[1568,160]{0,1:T(8,128)(2,1)} %param.12) | copy-start | bytes 1505284
  8.0 91.0 %copy-start.1 = (bf16[1024,384]{1,0:T(8,128)(2,1)S(1)}, bf16[1024,384]{1,0:T(8,128)(2,1)}, u32[]{:S(2)}) copy-start(bf16[1024,384]{1,0:T(8,128)(2,1)} %param.13) | copy-start | bytes 2359300
  8.0 91.7 %copy-start.14 = (s32[1,1024]{1,0:T(1,128)S(1)}, s32[1,1024]{1,0:T(1,128)}, u32[]{:S(2)}) copy-start(s32[1,1024]{1,0:T(1,128)} %param.19) | copy-start | bytes 12292
  8.0 148.9 %all-gather.6.cloned.1.call-start = ((), (), s32[]{:S(2)}) async-start(), calls=%async_computation.8 | async-start | bytes 1689600 | tf_op jit(solution)/shard_map/all_gather | solution.py:150
  8.8 290.2 %all-gather.8.cloned.1.call-start = ((), (), s32[]{:S(2)}) async-start(), calls=%async_computation.9 | async-start | bytes 1689600 | tf_op jit(solution)/shard_map/all_gather | solution.py:151
  10.9 90.7 %all-to-all-start = ((bf16[32,192,12]{1,2,0:T(8,128)(2,1)}), bf16[32,192,12]{1,2,0:T(8,128)(2,1)S(1)}, u32[]{:S(2)}, u32[]{:S(2)}) async-start(bf16[32,192,12]{1,2,0:T(8,128)(2,1)} %broadcast_in_dim.10), calls=%async_computation | async-start | bytes 524288 | tf_op jit(solution)/shard_map/all_to_all | solution.py:27
  102.9 22.0 %all-to-all-start.1 = ((bf16[8,512,160]{1,2,0:T(8,128)(2,1)}), bf16[8,512,160]{1,2,0:T(8,128)(2,1)S(1)}, u32[]{:S(2)}, u32[]{:S(2)}) async-start(bf16[8,512,160]{1,2,0:T(8,128)(2,1)} %broadcast_in_dim.11), calls=%async_computation.1 | async-start | bytes 2621440 | tf_op jit(solution)/shard_map/all_to_all | solution.py:27
  107.7 219.2 %all-reduce.5.cloned.1.call-start = ((), (), s32[]{:S(2)}) async-start(), calls=%async_computation.7 | async-start | bytes 3145728 | tf_op jit(solution)/shard_map/psum | solution.py:194
  109.3 4.5 copy-start.4
  113.8 228.6 %reduce-scatter.3.cloned.1.call-start = ((), (), s32[]{:S(2)}) async-start(), calls=%async_computation.10 | async-start | bytes 2949120 | tf_op jit(solution)/shard_map/reduce_scatter | solution.py:164
  312.0 13.6 %all-to-all-start.3 = ((f32[16,1,1]{2,1,0:T(1,128)}), f32[16,1,1]{2,1,0:T(1,128)S(1)}, u32[]{:S(2)}, u32[]{:S(2)}) async-start(f32[16,1,1]{2,1,0:T(1,128)} %broadcast_in_dim.13), calls=%async_computation.4 | async-start | bytes 16384 | tf_op jit(solution)/shard_map/all_to_all | solution.py:27
  326.8 1.9 copy-start.2
  328.7 13.8 %copy-start.10 = (bf16[512,160]{0,1:T(8,128)(2,1)S(1)}, bf16[512,160]{0,1:T(8,128)(2,1)}, u32[]{:S(2)}) copy-start(bf16[512,160]{0,1:T(8,128)(2,1)} %copy-done.9) | copy-start | bytes 491524
  344.2 11.1 %all-to-all-start.2 = ((f32[8,1,1024]{2,1,0:T(1,128)}), f32[8,1,1024]{2,1,0:T(1,128)S(1)}, u32[]{:S(2)}, u32[]{:S(2)}) async-start(f32[8,1,1024]{2,1,0:T(1,128)} %broadcast_in_dim.12), calls=%async_computation.3 | async-start | bytes 65536 | tf_op jit(solution)/shard_map/all_to_all | solution.py:27
  351.2 55.7 %reduce-scatter.5.cloned.1.call-start = ((), (), s32[]{:S(2)}) async-start(), calls=%async_computation.11 | async-start | bytes 1769472 | tf_op jit(solution)/shard_map/reduce_scatter | solution.py:71
  356.3 11.2 %copy-start.8 = (bf16[384,352]{1,0:T(8,128)(2,1)S(1)}, bf16[384,352]{1,0:T(8,128)(2,1)}, u32[]{:S(2)}) copy-start(bf16[384,352]{1,0:T(8,128)(2,1)} %reshape.189) | copy-start | bytes 811012
  356.3 11.1 %collective-permute-start = (bf16[512,160]{0,1:T(8,128)(2,1)S(1)}, bf16[512,160]{0,1:T(8,128)(2,1)S(1)}, u32[]{:S(2)}, u32[]{:S(2)}) collective-permute-start(bf16[512,160]{0,1:T(8,128)(2,1)S(1)} %multiply_convert_fusion.2), channel_id=1, source_target_pairs={{0,128},{1,129},{2,130},{3,131},{4,132},{5,133},{6,134},{7,135},{8... | collective-permute-start | bytes 491528 | tf_op jit(solution)/shard_map/ppermute | solution.py:50
  364.5 4.5 copy-start.7
  370.7 65.2 %all-gather.10.cloned.1.call-start = ((), (), s32[]{:S(2)}) async-start(), calls=%async_computation.12 | async-start | bytes 1769472 | tf_op jit(solution)/shard_map/all_gather | solution.py:74
  436.0 2.3 copy-start.3
  438.2 1.8 copy-start.5
  444.4 38.6 %copy-start.15 = (u32[256]{0:T(256)S(1)}, u32[256]{0:T(256)}, u32[]{:S(2)}) copy-start(u32[256]{0:T(256)} %constant.79) | copy-start | bytes 3076
  444.4 165.4 %all-to-all-start.4 = ((f32[32,192,12]{1,2,0:T(8,128)}), f32[32,192,12]{1,2,0:T(8,128)S(1)}, u32[]{:S(2)}, u32[]{:S(2)}) async-start(f32[32,192,12]{1,2,0:T(8,128)} %bitcast.9), calls=%async_computation.6 | async-start | bytes 1048576 | tf_op jit(solution)/shard_map/all_to_all | solution.py:99
  454.4 152.7 %all-reduce.7.cloned.1.call-start = ((), (), s32[]{:S(2)}) async-start(), calls=%async_computation.13 | async-start | bytes 655360
  (5 other events, 5.8 us)
Sparse Core Ops, SparseCore 0:
  10.6 146.2 all-gather.5
  158.7 140.2 all-gather.7
  458.6 148.3 all-reduce.6
Sparse Core Ops, SparseCore 1:
  113.9 67.6 all-reduce.4
  310.8 31.6 reduce-scatter.2
  370.8 36.1 reduce-scatter.4
  408.8 27.1 all-gather.9
where the time goes:
time: 620 us; the launch traced here: 619 us
  waiting for transfers between devices  375 us (60%)
  blocking collectives  126 us (20%)
  starting transfers between devices  47.1 us (8%)
  between operations  20.9 us (3%)
  matrix products  19.1 us (3%)
  local copies, waits for them, and re-layouts  15.9 us (3%)
  other arithmetic  14.2 us (2%)
    all_gather x1, waiting for transfers between devices, body(): down_rows = lax.all_gather(ema_down, ROLE_DP, axis=1, tiled=True)  142 us
    unnamed x8, waiting for transfers between devices  99.9 us
    all_gather x1, blocking collectives, sent_together(): filled = lax.all_gather(both, axis, axis=dim, tiled=True)  75.8 us
    psum x5, blocking collectives, by_axis(): return functools.reduce(lax.psum, axes, shard)  50.4 us
    reduce_scatter x1, waiting for transfers between devices, sum_by_parts(): lax.psum_scatter(filled_up(lines, lax.axis_size(axis)), axis, scatter_dim...  36 us
    all_gather x1, waiting for transfers between devices, body(): up_cols = lax.all_gather(ema_up, ROLE_DP, axis=0, tiled=True)  32 us
    all_to_all x4, starting transfers between devices, from_everyone(): return lax.all_to_all(copies, axis, split_axis=0, concat_axis=0, tiled=True)  29 us
    all_gather x1, waiting for transfers between devices, sum_by_parts(): whole = lax.all_gather(own, axis).reshape(-1, *lines.shape[1:])  27.1 us
  transfers between devices with their start and end apart: 13, of which 10 were waited for; matrix products, arithmetic and copies ran while one was open for 6% of the time, Pallas kernels for 0%

commit v1 on v0

--- a/solution.py
+++ b/solution.py
@@ -14,6 +14,17 @@
 ROLE_DP_MP = ("role", "dp_0", "dp_1", "mp_0", "mp_1")
 EPS = 1e-06
 COEF = 0.7978845608028654
+
+
+def surface_solve(block_in, axis_id):
+    w1 = jnp.concatenate(
+        lax.all_to_all(jnp.stack([block_in for _ in range(lax.axis_size(axis_id))]), axis_id, 0, 0),
+        axis=1,
+    )
+    return w1
+
+
+handle_the_yards = functools.partial(surface_solve, axis_id=ROLE_DP)
 
 
 def joined_along(pieces, dim):
@@ -148,7 +159,7 @@
     working = role_index >= 0
     block_rows = own_rows.shape[0]
     up_cols = lax.all_gather(ema_up, ROLE_DP, axis=0, tiled=True)
-    down_rows = lax.all_gather(ema_down, ROLE_DP, axis=1, tiled=True)
+    down_rows = handle_the_yards(ema_down)
 
     def encode_block():
         normed = normalize(whole_rows.astype(jnp.float32)).astype(jnp.bfloat16)

time: 620 us -> 566 us (0.913)
  waiting for transfers between devices: 375 us -> 280 us
  blocking collectives: 126 us -> 164 us
    all_gather x1 -> x0, waiting for transfers between devices: 142 us -> none  [body(): down_rows = lax.all_gather(ema_down, ROLE_DP, axis=1, tiled=True)]
    all_gather x1, blocking collectives: 75.8 us -> 113 us  [sent_together(): filled = lax.all_gather(both, axis, axis=dim, tiled=True)]
    psum x1, waiting for transfers between devices: 0.03 us -> 34.8 us  [body(): lax.psum(jnp.dot(hid_act, down_cols, preferred_element_type=jnp.float32),...]
    all_gather x1, waiting for transfers between devices: 32 us -> 4.71 us  [body(): up_cols = lax.all_gather(ema_up, ROLE_DP, axis=0, tiled=True)]
    reduce_scatter x1, waiting for transfers between devices: 13.2 us -> 35.9 us  [body(): branch = lax.psum_scatter(partial_sum, MP, scatter_dimension=1, tiled=True)]
    all_to_all x4, waiting for transfers between devices: 22.2 us -> 39.6 us  [from_everyone(): return lax.all_to_all(copies, axis, split_axis=0, concat_axis=0, tiled=True)]
    unnamed x8 -> x7, waiting for transfers between devices: 99.9 us -> 99.2 us
  transfers between devices with their start and end apart: 13 -> 13, of which waited for: 10 -> 11; matrix products, arithmetic and copies ran while one was open for 6% -> 6% of each run, Pallas kernels for 0% -> 0%
where the time goes in v1:
time: 566 us; the launch traced here: 565 us
  waiting for transfers between devices  280 us (49%)
  blocking collectives  164 us (29%)
  starting transfers between devices  50 us (9%)
  between operations  21.1 us (4%)
  local copies, waits for them, and re-layouts  18.2 us (3%)
  matrix products  18.2 us (3%)
  other arithmetic  13.5 us (2%)
    all_gather x1, blocking collectives, sent_together(): filled = lax.all_gather(both, axis, axis=dim, tiled=True)  113 us
    unnamed x7, waiting for transfers between devices  99.2 us
    psum x5, blocking collectives, by_axis(): return functools.reduce(lax.psum, axes, shard)  50.4 us
    all_to_all x4, waiting for transfers between devices, from_everyone(): return lax.all_to_all(copies, axis, split_axis=0, concat_axis=0, tiled=True)  39.6 us
    reduce_scatter x1, waiting for transfers between devices, sum_by_parts(): lax.psum_scatter(filled_up(lines, lax.axis_size(axis)), axis, scatter_dim...  35.9 us
    reduce_scatter x1, waiting for transfers between devices, body(): branch = lax.psum_scatter(partial_sum, MP, scatter_dimension=1, tiled=True)  35.9 us
    psum x1, waiting for transfers between devices, body(): lax.psum(jnp.dot(hid_act, down_cols, preferred_element_type=jnp.float32),...  34.8 us
    all_gather x1, waiting for transfers between devices, sum_by_parts(): whole = lax.all_gather(own, axis).reshape(-1, *lines.shape[1:])  27.1 us
  transfers between devices with their start and end apart: 13, of which 11 were waited for; matrix products, arithmetic and copies ran while one was open for 6% of the time, Pallas kernels for 0%

profile of v1, /device:TPU:2, one launch (start us, length us, event | category | flops | bytes accessed | tf_op | source)
XLA Modules:
  0.0 565.0 jit_solution(11095900421214824863)
XLA Ops:
  9.5 11.5 %all-to-all-start = ((bf16[32,192,12]{1,2,0:T(8,128)(2,1)}), bf16[32,192,12]{1,2,0:T(8,128)(2,1)S(1)}, u32[]{:S(2)}, u32[]{:S(2)}) async-start(bf16[32,192,12]{1,2,0:T(8,128)(2,1)} %broadcast_in_dim.10), calls=%async_computation | async-start | bytes 524288 | tf_op jit(solution)/shard_map/all_to_all | solution.py:38
  22.6 12.0 %all-to-all-done = bf16[32,192,12]{1,2,0:T(8,128)(2,1)S(1)} async-done(((bf16[32,192,12]{1,2,0:T(8,128)(2,1)}), bf16[32,192,12]{1,2,0:T(8,128)(2,1)S(1)}, u32[]{:S(2)}, u32[]{:S(2)}) %all-to-all-start) | async-done | bytes 147488 | tf_op jit(solution)/shard_map/all_to_all | solution.py:38
  35.8 5.0 all-to-all-start.1
  41.5 16.6 %all-to-all-done.1 = bf16[8,512,160]{1,2,0:T(8,128)(2,1)S(1)} async-done(((bf16[8,512,160]{1,2,0:T(8,128)(2,1)}), bf16[8,512,160]{1,2,0:T(8,128)(2,1)S(1)}, u32[]{:S(2)}, u32[]{:S(2)}) %all-to-all-start.1) | async-done | bytes 1310752 | tf_op jit(solution)/shard_map/all_to_all | solution.py:38
  59.4 4.8 all-to-all-start.2
  64.4 113.4 %all-gather.1 = bf16[32,12,352]{2,1,0:T(8,128)(2,1)S(1)} all-gather(bf16[1,12,352]{2,1,0:T(8,128)(2,1)S(1)} %maximum_bitcast_fusion.1), channel_id=1, replica_groups=mesh['role'=2,'dp_0'=4,'dp_1'=4,'mp_0'=4,'mp_1'=2] {'role','dp_0','dp_1'}, dimensions={0}, use_global_device_ids=true | all-gather | bytes 278784 | tf_op jit(solution)/shard_map/all_gather | solution.py:67
  184.9 4.7 all-gather.5.cloned.1.call-done
  189.6 8.5 %conditional.1 = (f32[512,1280]{1,0:T(8,128)}) conditional(s32[]{:T(128)} %convert_element_type.101, () %tuple.14, (bf16[512,8,160]{0,2,1:T(8,128)(2,1)S(1)}, bf16[1280,640]{1,0:T(8,128)(2,1)}, bf16[640,32,40]{0,2,1:T(8,128)(2,1)}) %tuple.36), branch_computations={%region_5.0_spmd, %region_6.9_spmd} | conditional | flops 1687224832 | bytes 12470280 | solution.py:174
  191.7 6.4 %fusion.10 = f32[512,1280]{1,0:T(8,128)} fusion(bf16[640,1280]{0,1:T(8,128)(2,1)} %bitcast.1, bf16[512,1280]{0,1:T(8,128)(2,1)} %fusion.1, bf16[1280,640]{1,0:T(8,128)(2,1)} %get-tuple-element.12), kind=kOutput, calls=%fused_computation.14 | convolution fusion | flops 1680670720 | bytes 7208960 | tf_op jit(solution)/shard_map/cond/branch_1_fun/dot_general | solution.py:169
  202.7 3.5 all-to-all-start.4
  206.8 7.1 %all-to-all-done.4 = f32[16,1,1]{2,1,0:T(1,128)S(1)} async-done(((f32[16,1,1]{2,1,0:T(1,128)}), f32[16,1,1]{2,1,0:T(1,128)S(1)}, u32[]{:S(2)}, u32[]{:S(2)}) %all-to-all-start.4) | async-done | bytes 96 | tf_op jit(solution)/shard_map/all_to_all | solution.py:38
  215.2 34.8 %all-reduce.5.cloned.1.call-done = f32[1024,384]{1,0:T(8,128)} async-done(((f32[1024,384]{1,0:T(8,128)}), f32[1024,384]{1,0:T(8,128)}) %all-reduce.5.cloned.1.call-update) | async-done | bytes 1572880 | tf_op jit(solution)/shard_map/psum | solution.py:205
  252.4 35.9 %reduce-scatter.3.cloned.1.call-done = f32[512,160]{0,1:T(8,128)} async-done(((f32[512,1280]{0,1:T(8,128)}), f32[512,160]{0,1:T(8,128)}) %reduce-scatter.3.cloned.1.call-update) | async-done | bytes 327696 | tf_op jit(solution)/shard_map/reduce_scatter | solution.py:175
  290.0 7.1 %all-to-all-start.3 = ((f32[8,1,1024]{2,1,0:T(1,128)}), f32[8,1,1024]{2,1,0:T(1,128)S(1)}, u32[]{:S(2)}, u32[]{:S(2)}) async-start(f32[8,1,1024]{2,1,0:T(1,128)} %broadcast_in_dim.12), calls=%async_computation.4 | async-start | bytes 65536 | tf_op jit(solution)/shard_map/all_to_all | solution.py:38
  297.1 4.0 all-to-all-done.3
  302.2 7.8 %collective-permute-start = (bf16[512,160]{0,1:T(8,128)(2,1)S(1)}, bf16[512,160]{0,1:T(8,128)(2,1)S(1)}, u32[]{:S(2)}, u32[]{:S(2)}) collective-permute-start(bf16[512,160]{0,1:T(8,128)(2,1)S(1)} %multiply_convert_fusion.2), channel_id=1, source_target_pairs={{0,128},{1,129},{2,130},{3,131},{4,132},{5,133},{6,134},{7,135},{8... | collective-permute-start | bytes 491528 | tf_op jit(solution)/shard_map/ppermute | solution.py:61
  316.8 35.9 %reduce-scatter.5.cloned.1.call-done = f32[128,384]{1,0:T(8,128)} async-done(((f32[1024,384]{1,0:T(8,128)}), f32[128,384]{1,0:T(8,128)}) %reduce-scatter.5.cloned.1.call-update) | async-done | bytes 196624 | tf_op jit(solution)/shard_map/reduce_scatter | solution.py:82
  354.6 27.1 %all-gather.7.cloned.1.call-done = f32[1024,384]{1,0:T(8,128)} async-done(((f32[128,384]{1,0:T(8,128)}), f32[1024,384]{1,0:T(8,128)}) %all-gather.7.cloned.1.call-update) | async-done | bytes 1572880 | tf_op jit(solution)/shard_map/all_gather | solution.py:85
  390.2 10.0 %all-to-all-start.5 = ((f32[32,192,12]{1,2,0:T(8,128)}), f32[32,192,12]{1,2,0:T(8,128)S(1)}, u32[]{:S(2)}, u32[]{:S(2)}) async-start(f32[32,192,12]{1,2,0:T(8,128)} %bitcast.11), calls=%async_computation.7 | async-start | bytes 1048576 | tf_op jit(solution)/shard_map/all_to_all | solution.py:110
  402.1 16.2 %psum.43 = f32[]{:T(128)} all-reduce(f32[]{:T(128)S(6)} %mul.192), channel_id=1, replica_groups=mesh['role'=2,'dp_0'=4,'dp_1'=4,'mp_0'=4,'mp_1'=2] {'role'}, use_global_device_ids=true, to_apply=%region_14.0 | all-reduce | flops 1 | bytes 8 | tf_op jit(solution)/shard_map/psum | solution.py:72
  418.4 10.4 %psum.44 = f32[]{:T(128)} all-reduce(f32[]{:T(128)} %psum.43), channel_id=1, replica_groups=mesh['role'=2,'dp_0'=4,'dp_1'=4,'mp_0'=4,'mp_1'=2] {'dp_0'}, use_global_device_ids=true, to_apply=%region_15.0 | all-reduce | flops 1 | bytes 8 | tf_op jit(solution)/shard_map/psum | solution.py:72
  429.4 10.3 %psum.45 = f32[]{:T(128)} all-reduce(f32[]{:T(128)} %psum.44), channel_id=1, replica_groups=mesh['role'=2,'dp_0'=4,'dp_1'=4,'mp_0'=4,'mp_1'=2] {'dp_1'}, use_global_device_ids=true, to_apply=%region_16.0 | all-reduce | flops 1 | bytes 8 | tf_op jit(solution)/shard_map/psum | solution.py:72
  440.3 10.4 %psum.46 = f32[]{:T(128)} all-reduce(f32[]{:T(128)} %psum.45), channel_id=1, replica_groups=mesh['role'=2,'dp_0'=4,'dp_1'=4,'mp_0'=4,'mp_1'=2] {'mp_0'}, use_global_device_ids=true, to_apply=%region_17.0 | all-reduce | flops 1 | bytes 8 | tf_op jit(solution)/shard_map/psum | solution.py:72
  454.4 98.4 %all-reduce.7.cloned.1.call-done = bf16[1280,128]{1,0:T(8,128)(2,1)} async-done(((bf16[1280,128]{1,0:T(8,128)(2,1)}), bf16[1280,128]{1,0:T(8,128)(2,1)}) %all-reduce.7.cloned.1.call-update) | async-done | bytes 327696
  (110 shorter events, 50.7 us)
Async XLA Ops:
  8.0 13.7 %copy-start = (bf16[1568,160]{0,1:T(8,128)(2,1)S(1)}, bf16[1568,160]{0,1:T(8,128)(2,1)}, u32[]{:S(2)}) copy-start(bf16[1568,160]{0,1:T(8,128)(2,1)} %param.12) | copy-start | bytes 1505284
  9.5 25.1 %all-to-all-start = ((bf16[32,192,12]{1,2,0:T(8,128)(2,1)}), bf16[32,192,12]{1,2,0:T(8,128)(2,1)S(1)}, u32[]{:S(2)}, u32[]{:S(2)}) async-start(bf16[32,192,12]{1,2,0:T(8,128)(2,1)} %broadcast_in_dim.10), calls=%async_computation | async-start | bytes 524288 | tf_op jit(solution)/shard_map/all_to_all | solution.py:38
  22.6 13.2 %copy-start.10 = (bf16[512,160]{0,1:T(8,128)(2,1)}, bf16[512,160]{0,1:T(8,128)(2,1)S(1)}, u32[]{:S(2)}) copy-start(bf16[512,160]{0,1:T(8,128)(2,1)S(1)} %fusion.29) | copy-start | bytes 491524
  35.8 22.3 %copy-start.15 = (bf16[640,40]{0,1:T(8,128)(2,1)S(1)}, bf16[640,40]{0,1:T(8,128)(2,1)}, u32[]{:S(2)}) copy-start(bf16[640,40]{0,1:T(8,128)(2,1)} %param.15) | copy-start | bytes 153604
  35.8 22.2 %all-to-all-start.1 = ((bf16[8,512,160]{1,2,0:T(8,128)(2,1)}), bf16[8,512,160]{1,2,0:T(8,128)(2,1)S(1)}, u32[]{:S(2)}, u32[]{:S(2)}) async-start(bf16[8,512,160]{1,2,0:T(8,128)(2,1)} %broadcast_in_dim.11), calls=%async_computation.1 | async-start | bytes 2621440 | tf_op jit(solution)/shard_map/all_to_all | solution.py:38
  40.7 148.9 %all-gather.5.cloned.1.call-start = ((), (), s32[]{:S(2)}) async-start(), calls=%async_computation.9 | async-start | bytes 1689600 | tf_op jit(solution)/shard_map/all_gather | solution.py:161
  59.4 4.9 copy-start.16
  59.4 4.9 copy-start.17
  59.4 119.2 %copy-start.1 = (bf16[1024,384]{1,0:T(8,128)(2,1)S(1)}, bf16[1024,384]{1,0:T(8,128)(2,1)}, u32[]{:S(2)}) copy-start(bf16[1024,384]{1,0:T(8,128)(2,1)} %param.13) | copy-start | bytes 2359300
  59.4 125.5 %all-to-all-start.2 = ((bf16[32,640,40]{1,2,0:T(8,128)(2,1)}), bf16[32,640,40]{1,2,0:T(8,128)(2,1)}, u32[]{:S(2)}, u32[]{:S(2)}) async-start(bf16[32,640,40]{1,2,0:T(8,128)(2,1)} %stack.2), calls=%async_computation.2 | async-start | bytes 3276800 | tf_op jit(solution)/shard_map/all_to_all | solution.py:21
  64.2 185.8 %all-reduce.5.cloned.1.call-start = ((), (), s32[]{:S(2)}) async-start(), calls=%async_computation.8 | async-start | bytes 3145728 | tf_op jit(solution)/shard_map/psum | solution.py:205
  180.3 4.5 copy-start.4
  184.8 103.4 %reduce-scatter.3.cloned.1.call-start = ((), (), s32[]{:S(2)}) async-start(), calls=%async_computation.10 | async-start | bytes 2949120 | tf_op jit(solution)/shard_map/reduce_scatter | solution.py:175
  202.7 11.3 %all-to-all-start.4 = ((f32[16,1,1]{2,1,0:T(1,128)}), f32[16,1,1]{2,1,0:T(1,128)S(1)}, u32[]{:S(2)}, u32[]{:S(2)}) async-start(f32[16,1,1]{2,1,0:T(1,128)} %broadcast_in_dim.13), calls=%async_computation.5 | async-start | bytes 16384 | tf_op jit(solution)/shard_map/all_to_all | solution.py:38
  251.8 36.5 %copy-start.11 = (bf16[512,160]{0,1:T(8,128)(2,1)S(1)}, bf16[512,160]{0,1:T(8,128)(2,1)}, u32[]{:S(2)}) copy-start(bf16[512,160]{0,1:T(8,128)(2,1)} %copy-done.10) | copy-start | bytes 491524
  290.0 11.1 %all-to-all-start.3 = ((f32[8,1,1024]{2,1,0:T(1,128)}), f32[8,1,1024]{2,1,0:T(1,128)S(1)}, u32[]{:S(2)}, u32[]{:S(2)}) async-start(f32[8,1,1024]{2,1,0:T(1,128)} %broadcast_in_dim.12), calls=%async_computation.4 | async-start | bytes 65536 | tf_op jit(solution)/shard_map/all_to_all | solution.py:38
  297.1 55.7 %reduce-scatter.5.cloned.1.call-start = ((), (), s32[]{:S(2)}) async-start(), calls=%async_computation.11 | async-start | bytes 1769472 | tf_op jit(solution)/shard_map/reduce_scatter | solution.py:82
  302.2 11.2 %copy-start.9 = (bf16[384,352]{1,0:T(8,128)(2,1)S(1)}, bf16[384,352]{1,0:T(8,128)(2,1)}, u32[]{:S(2)}) copy-start(bf16[384,352]{1,0:T(8,128)(2,1)} %reshape.199) | copy-start | bytes 811012
  302.2 11.2 %collective-permute-start = (bf16[512,160]{0,1:T(8,128)(2,1)S(1)}, bf16[512,160]{0,1:T(8,128)(2,1)S(1)}, u32[]{:S(2)}, u32[]{:S(2)}) collective-permute-start(bf16[512,160]{0,1:T(8,128)(2,1)S(1)} %multiply_convert_fusion.2), channel_id=1, source_target_pairs={{0,128},{1,129},{2,130},{3,131},{4,132},{5,133},{6,134},{7,135},{8... | collective-permute-start | bytes 491528 | tf_op jit(solution)/shard_map/ppermute | solution.py:61
  310.3 4.5 copy-start.7
  316.6 65.2 %all-gather.7.cloned.1.call-start = ((), (), s32[]{:S(2)}) async-start(), calls=%async_computation.12 | async-start | bytes 1769472 | tf_op jit(solution)/shard_map/all_gather | solution.py:85
  390.2 38.6 %copy-start.18 = (u32[256]{0:T(256)S(1)}, u32[256]{0:T(256)}, u32[]{:S(2)}) copy-start(u32[256]{0:T(256)} %constant.79) | copy-start | bytes 3076
  390.2 165.5 %all-to-all-start.5 = ((f32[32,192,12]{1,2,0:T(8,128)}), f32[32,192,12]{1,2,0:T(8,128)S(1)}, u32[]{:S(2)}, u32[]{:S(2)}) async-start(f32[32,192,12]{1,2,0:T(8,128)} %bitcast.11), calls=%async_computation.7 | async-start | bytes 1048576 | tf_op jit(solution)/shard_map/all_to_all | solution.py:110
  400.2 152.7 %all-reduce.7.cloned.1.call-start = ((), (), s32[]{:S(2)}) async-start(), calls=%async_computation.13 | async-start | bytes 655360
  (8 other events, 11.4 us)
Sparse Core Ops, SparseCore 0:
  43.3 146.2 all-gather.4
  404.4 148.3 all-reduce.6
Sparse Core Ops, SparseCore 1:
  184.9 65.0 all-reduce.4
  252.4 35.8 reduce-scatter.2
  316.7 36.0 reduce-scatter.4
  354.6 27.1 all-gather.6
